TPU v7x, 256 devices: a whole 4x4x8 slice. The times are simulated.
256 devices in a mesh: row: 16 (over z, y_hi), col: 4 (over x), depth: 4 (over y_lo, core).
Axes of the slice: x: 4, y: 4 (y_hi: 2, y_lo: 2; y = y_hi * 2 + y_lo), z: 8, core: 2. Of those that a mesh axis runs over, the one named last changes fastest.
Arguments:
- pair: bfloat16 [768, 768, 128], P('row', 'col'), may hold values from -6 to 6
- ln_gain: float32 [128], replicated, may hold values from 0.1 to 1.9
- ln_shift: float32 [128], replicated, may hold values from -3 to 3
- proj_weight: bfloat16 [128, 512], replicated, may hold values from -0.5 to 0.5
- proj_bias: float32 [512], replicated, may hold values from -3 to 3
- gate_weight: bfloat16 [128, 128], replicated, may hold values from -0.5 to 0.5
- gate_bias: float32 [128], replicated, may hold values from -3 to 3
- out_gain: float32 [128], replicated, may hold values from 0.1 to 1.9
- out_shift: float32 [128], replicated, may hold values from -3 to 3
- out_weight: bfloat16 [128, 128], replicated, may hold values from -0.5 to 0.5
- out_bias: float32 [128], replicated, may hold values from -3 to 3
Outputs:
- update: bfloat16 [768, 768, 128], P('row', 'col')
All inputs are finite; a program needn't handle non-finite values.
Results may differ from a plain program's by a relative error of at most 0.0051.
Values may be sent and summed in bfloat16 or wider, within the bound.
A program may use at most 128 MiB of HBM per device.

v0:
```python
import jax
import jax.numpy as jnp
from jax import lax
from jax.sharding import Mesh
from jax.sharding import PartitionSpec as P

ROW = ("row_0", "row_1")


def gather_axes(shard, axes, dim):
    for axis in reversed(axes):
        shard = lax.all_gather(shard, axis, axis=dim, tiled=True)
    return shard


def cut_along(shard, dim, count):
    lengths = shard.shape
    tiles = shard.reshape(*lengths[:dim], count, lengths[dim] // count, *lengths[dim + 1 :])
    return jnp.moveaxis(tiles, dim, 0)


def piece_ends(length, count):
    unit = 8 if length >= 8 * count else 1
    return [length // unit * k // count * unit for k in range(1, count)]


def laid_out(tiles, dim):
    lengths = list(tiles.shape[1:])
    lengths[dim] *= tiles.shape[0]
    return jnp.moveaxis(tiles, 0, dim).reshape(lengths)


def cut_exchange(shard, axis, pieces, split_dim, concat_dim):
    tiles = cut_along(shard, split_dim, lax.axis_size(axis))
    widest = max(range(1, max(2, tiles.ndim - 1)), key=lambda d: tiles.shape[d])
    done = []
    for share in jnp.split(tiles, piece_ends(tiles.shape[widest], pieces), axis=widest):
        if share.size:
            done.append(lax.all_to_all(share, axis, split_axis=0, concat_axis=0, tiled=True))
    return laid_out(jnp.concatenate(done, axis=widest), concat_dim)


def layer_norm(values, gain, shift):
    centre = jnp.mean(values, axis=-1, keepdims=True)
    centred = values - centre
    spread = jnp.mean(centred * centred, axis=-1, keepdims=True)
    return centred * lax.rsqrt(spread + 1e-05) * gain + shift


def project(piece, ln_gain, ln_shift, proj_weight, proj_bias, gate_weight, gate_bias):
    hidden = proj_weight.shape[1] // 4
    channels = piece.shape[2]
    normed = layer_norm(piece.astype(jnp.float32), ln_gain, ln_shift).astype(jnp.bfloat16)
    flat = normed.reshape(-1, channels)
    mixed = jnp.dot(flat, proj_weight, preferred_element_type=jnp.float32) + proj_bias
    left = (jax.nn.sigmoid(mixed[:, :hidden]) * mixed[:, hidden : 2 * hidden]).astype(jnp.bfloat16)
    right = (jax.nn.sigmoid(mixed[:, 2 * hidden : 3 * hidden]) * mixed[:, 3 * hidden :]).astype(
        jnp.bfloat16
    )
    gate = jax.nn.sigmoid(
        jnp.dot(flat, gate_weight, preferred_element_type=jnp.float32) + gate_bias
    )
    shape = (piece.shape[0], piece.shape[1])
    return (
        left.reshape(shape + (hidden,)),
        right.reshape(shape + (hidden,)),
        gate.reshape(shape + (channels,)),
    )


def finish(triangle, gate, out_gain, out_shift, out_weight, out_bias):
    hidden = triangle.shape[2]
    tri_normed = layer_norm(triangle, out_gain, out_shift).astype(jnp.bfloat16)
    projected = (
        jnp.dot(tri_normed.reshape(-1, hidden), out_weight, preferred_element_type=jnp.float32)
        + out_bias
    )
    return (gate * projected.reshape(gate.shape)).astype(jnp.bfloat16)


def per_device(
    pair,
    ln_gain,
    ln_shift,
    proj_weight,
    proj_bias,
    gate_weight,
    gate_bias,
    out_gain,
    out_shift,
    out_weight,
    out_bias,
):
    depth_count = lax.axis_size("depth")
    depth_id = lax.axis_index("depth")
    cols_here = pair.shape[1]
    quarter = cols_here // depth_count
    piece = lax.dynamic_slice_in_dim(pair, depth_id * quarter, quarter, 1)
    left, right, gate = project(
        piece, ln_gain, ln_shift, proj_weight, proj_bias, gate_weight, gate_bias
    )
    left_all = lax.all_gather(left, ("col", "depth"), axis=1, tiled=True)
    right_column = gather_axes(right, ROW, 0)
    needed = cut_exchange(right_column, ("col", "depth"), 2, 0, 1)
    triangle = jnp.einsum("ikc,jkc->ijc", left_all, needed, preferred_element_type=jnp.float32)
    finished = finish(triangle, gate, out_gain, out_shift, out_weight, out_bias)
    return lax.all_gather(finished, "depth", axis=1, tiled=True)


def solution(mesh):
    torus = Mesh(
        mesh.devices.reshape(8, 2, mesh.shape["col"], mesh.shape["depth"]),
        ("row_0", "row_1", "col", "depth"),
    )
    in_specs = (P(ROW, "col", None), P(), P(), P(), P(), P(), P(), P(), P(), P(), P())
    out_specs = P(ROW, "col", None)
    return jax.shard_map(
        per_device, mesh=torus, in_specs=in_specs, out_specs=out_specs, check_vma=False
    )
```

profile of v0, /device:TPU:5, one launch (start us, length us, event | category | flops | bytes accessed | tf_op | source)
XLA Modules:
  0.0 418.6 jit_solution(13620025771070307799)
XLA Ops:
  6.5 0.0 copy-start
  6.5 0.0 copy-start.4
  6.5 0.0 all-gather.5.cloned.1.call-start
  6.5 1.5 convert_reduce_fusion
  8.0 1.8 fusion.8
  9.8 1.8 fusion.11
  11.6 0.0 copy-done
  11.6 0.0 copy-done.4
  11.7 0.8 convolution_add_fusion
  12.4 1.4 fusion.12
  13.9 0.0 all-gather.5.cloned.1.call-update
  13.9 0.0 all-gather.7.cloned.1.call-start
  13.9 32.2 %all-gather.5.cloned.1.call-done = bf16[96,48,128]{2,1,0:T(8,128)(2,1)} async-done(((bf16[48,48,128]{2,1,0:T(8,128)(2,1)}), bf16[96,48,128]{2,1,0:T(8,128)(2,1)}) %all-gather.5.cloned.1.call-update) | async-done | bytes 1179664 | tf_op jit(solution)/shard_map/all_gather | solution.py:12
  46.2 0.0 all-gather.7.cloned.1.call-update
  46.2 0.0 all-gather.9.cloned.1.call-start
  46.2 1.0 copy.36
  47.2 0.0 all-gather.9.cloned.1.call-update
  47.2 104.1 %all-gather.7.cloned.1.call-done = bf16[768,48,128]{2,1,0:T(8,128)(2,1)} async-done(((bf16[96,48,128]{2,1,0:T(8,128)(2,1)}), bf16[768,48,128]{2,1,0:T(8,128)(2,1)}) %all-gather.7.cloned.1.call-update) | async-done | bytes 9437200 | tf_op jit(solution)/shard_map/all_gather | solution.py:12
  151.3 7.8 %fusion.20 = (bf16[16,24,48,128]{3,2,1,0:T(8,128)(2,1)S(1)}, bf16[16,24,48,128]{3,2,1,0:T(8,128)(2,1)}) fusion(bf16[16,48,48,128]{3,2,1,0:T(8,128)(2,1)} %bitcast.25), kind=kLoop, calls=%fused_computation.38 | loop fusion | bytes 18874368 | tf_op jit(solution)/shard_map/split | solution.py:37
  159.1 91.9 %all_to_all.10 = bf16[16,24,48,128]{3,2,1,0:T(8,128)(2,1)} all-to-all(bf16[16,24,48,128]{3,2,1,0:T(8,128)(2,1)S(1)} %get-tuple-element.5), channel_id=1, replica_groups=mesh['row_0'=8,'row_1'=2,'col'=4,'depth'=4] {'col','depth'}, dimensions={0} | all-to-all | bytes 9437184 | tf_op jit(solution)/shard_map/all_to_all | solution.py:39
  251.1 0.0 copy-start.8
  251.1 0.0 copy-start.9
  251.1 8.0 %all-to-all-start.1 = ((bf16[16,24,48,128]{3,2,1,0:T(8,128)(2,1)}), bf16[16,24,48,128]{3,2,1,0:T(8,128)(2,1)}, u32[]{:S(2)}, u32[]{:S(2)}) async-start(bf16[16,24,48,128]{3,2,1,0:T(8,128)(2,1)} %get-tuple-element.6), calls=%async_computation.1 | async-start | bytes 9437184 | tf_op jit(solution)/shard_map/all_to_all | solution.py:39
  259.0 0.2 all-gather.11.cloned.1.call-start
  259.3 0.0 copy-done.8
  259.3 0.0 copy-done.9
  259.3 1.5 fusion.4
  260.8 1.3 all-gather.9.cloned.1.call-done
  262.1 14.1 %copy.38 = bf16[48,768,128]{1,0,2:T(8,128)(2,1)} copy(bf16[48,768,128]{2,0,1:T(8,128)(2,1)} %all-gather.9.cloned.1.call-done) | data formatting | bytes 18874368 | tf_op jit(solution)/shard_map/all_gather | solution.py:102
  276.2 44.6 %all-to-all-done.1 = bf16[16,24,48,128]{3,2,1,0:T(8,128)(2,1)} async-done(((bf16[16,24,48,128]{3,2,1,0:T(8,128)(2,1)}), bf16[16,24,48,128]{3,2,1,0:T(8,128)(2,1)}, u32[]{:S(2)}, u32[]{:S(2)}) %all-to-all-start.1) | async-done | bytes 4718624 | tf_op jit(solution)/shard_map/all_to_all | solution.py:39
  320.8 7.6 %maximum_bitcast_fusion = bf16[48,16,48,128]{3,2,0,1:T(8,128)(2,1)} fusion(bf16[16,24,48,128]{3,2,1,0:T(8,128)(2,1)} %all-to-all-done.1, bf16[16,24,48,128]{3,2,1,0:T(8,128)(2,1)} %all_to_all.10), kind=kLoop, calls=%fused_computation | loop fusion | flops 4718592 | bytes 18874368 | tf_op jit(solution)/shard_map/transpose | solution.py:30
  328.4 10.1 %copy.35 = bf16[48,16,48,128]{3,2,1,0:T(8,128)(2,1)} copy(bf16[48,16,48,128]{3,2,0,1:T(8,128)(2,1)} %maximum_bitcast_fusion) | data formatting | bytes 18874368 | tf_op jit(solution)/shard_map/transpose | solution.py:30
  338.5 12.8 %copy.37 = bf16[48,768,128]{1,0,2:T(8,128)(2,1)} copy(bf16[48,768,128]{2,1,0:T(8,128)(2,1)} %bitcast.24) | data formatting | bytes 18874368 | tf_op jit(solution)/shard_map/reshape | solution.py:30
  351.3 9.0 %bitcast_reduce_fusion = (f32[48,48]{0,1:T(8,128)S(1)}, f32[128,48,48]{2,1,0:T(8,128)S(1)}) fusion(bf16[48,768,128]{1,0,2:T(8,128)(2,1)} %copy.37, bf16[48,768,128]{1,0,2:T(8,128)(2,1)} %copy.38), kind=kOutput, calls=%fused_computation.11 | convolution fusion | flops 453277440 | bytes 20063232 | tf_op jit(solution)/shard_map/ikc,jkc->ijc/dot_general | solution.py:105
  360.3 0.0 copy-start.6
  360.3 0.0 copy-start.7
  360.3 0.1 copy.39
  360.4 0.1 copy.40
  360.5 0.5 multiply_reduce_fusion
  361.0 0.1 copy.41
  361.1 0.1 copy.42
  361.1 0.0 copy-done.6
  361.1 0.0 copy-done.7
  361.2 0.0 copy-start.3
  361.2 0.0 copy-start.5
  361.2 1.7 add_convert_fusion
  362.9 0.0 copy-start.2
  362.9 2.4 copy.43
  365.3 0.0 copy-done.3
  365.3 0.0 copy-done.5
  365.3 0.0 copy-done.2
  365.3 1.1 fusion.5
  366.4 0.0 all-gather.11.cloned.1.call-update
  366.4 0.0 copy-start.1
  366.4 42.4 %all-gather.11.cloned.1.call-done = bf16[48,192,128]{2,1,0:T(8,128)(2,1)} async-done(((bf16[48,48,128]{2,1,0:T(8,128)(2,1)}), bf16[48,192,128]{2,1,0:T(8,128)(2,1)}) %all-gather.11.cloned.1.call-update) | async-done | bytes 2359312 | tf_op jit(solution)/shard_map/all_gather | solution.py:107
  408.8 3.2 copy.45
  412.0 0.0 copy-done.1
  (4 shorter events, 0.0 us)
Async XLA Ops:
  6.5 5.1 %copy-start = (bf16[128,512]{1,0:T(8,128)(2,1)S(1)}, bf16[128,512]{1,0:T(8,128)(2,1)}, u32[]{:S(2)}) copy-start(bf16[128,512]{1,0:T(8,128)(2,1)} %param.14) | copy-start | bytes 393220
  6.5 5.1 %copy-start.4 = (f32[512]{0:T(512)S(1)}, f32[512]{0:T(512)}, u32[]{:S(2)}) copy-start(f32[512]{0:T(512)} %param.15) | copy-start | bytes 6148
  6.5 39.6 %all-gather.5.cloned.1.call-start = ((), (), s32[]{:S(2)}) async-start(), calls=%async_computation.2 | async-start | bytes 1769472 | tf_op jit(solution)/shard_map/all_gather | solution.py:12
  13.9 137.4 %all-gather.7.cloned.1.call-start = ((), (), s32[]{:S(2)}) async-start(), calls=%async_computation.3 | async-start | bytes 10616832 | tf_op jit(solution)/shard_map/all_gather | solution.py:12
  46.2 215.9 %all-gather.9.cloned.1.call-start = ((), (), s32[]{:S(2)}) async-start(), calls=%async_computation.4 | async-start | bytes 10027008 | tf_op jit(solution)/shard_map/all_gather | solution.py:102
  251.1 8.2 %copy-start.8 = (bf16[128,128]{1,0:T(8,128)(2,1)S(1)}, bf16[128,128]{1,0:T(8,128)(2,1)}, u32[]{:S(2)}) copy-start(bf16[128,128]{1,0:T(8,128)(2,1)} %param.16) | copy-start | bytes 98308
  251.1 8.2 %copy-start.9 = (f32[128]{0:T(128)S(1)}, f32[128]{0:T(128)}, u32[]{:S(2)}) copy-start(f32[128]{0:T(128)} %param.17) | copy-start | bytes 1540
  251.1 69.7 %all-to-all-start.1 = ((bf16[16,24,48,128]{3,2,1,0:T(8,128)(2,1)}), bf16[16,24,48,128]{3,2,1,0:T(8,128)(2,1)}, u32[]{:S(2)}, u32[]{:S(2)}) async-start(bf16[16,24,48,128]{3,2,1,0:T(8,128)(2,1)} %get-tuple-element.6), calls=%async_computation.1 | async-start | bytes 9437184 | tf_op jit(solution)/shard_map/all_to_all | solution.py:39
  259.0 149.8 %all-gather.11.cloned.1.call-start = ((), (), s32[]{:S(2)}) async-start(), calls=%async_computation.5 | async-start | bytes 2949120 | tf_op jit(solution)/shard_map/all_gather | solution.py:107
  360.3 0.8 copy-start.6
  360.3 0.8 copy-start.7
  361.2 4.1 copy-start.3
  361.2 4.1 copy-start.5
  362.9 2.4 copy-start.2
  366.4 45.6 %copy-start.1 = (bf16[128,512]{1,0:T(8,128)(2,1)S(1)}, bf16[128,512]{1,0:T(8,128)(2,1)}, u32[]{:S(2)}) copy-start(bf16[128,512]{1,0:T(8,128)(2,1)} %param.14) | copy-start | bytes 393220
Sparse Core Ops, SparseCore 0:
  14.0 32.1 all-gather.4
  47.9 103.3 all-gather.6
  153.2 108.8 all-gather.8
  366.6 42.2 all-gather.10
where the time goes:
time: 420 us; the launch traced here: 419 us
  waiting for transfers between devices  225 us (54%)
  blocking collectives  91.9 us (22%)
  local copies, waits for them, and re-layouts  51.8 us (12%)
  other arithmetic  16.3 us (4%)
  between operations  13.3 us (3%)
  matrix products  12.3 us (3%)
  starting transfers between devices  8.26 us (2%)
    all_gather x2, waiting for transfers between devices, gather_axes(): shard = lax.all_gather(shard, axis, axis=dim, tiled=True)  136 us
    all_to_all x1, blocking collectives, cut_exchange(): lax.all_to_all(share, axis, split_axis=0, concat_axis=0, tiled=True)  91.9 us
    all_to_all x1, waiting for transfers between devices, cut_exchange(): lax.all_to_all(share, axis, split_axis=0, concat_axis=0, tiled=True)  44.6 us
    all_gather x1, waiting for transfers between devices, per_device(): return lax.all_gather(finished, 'depth', axis=1, tiled=True)  42.4 us
    all_gather x1, local copies, waits for them, and re-layouts, per_device(): left_all = lax.all_gather(left, ('col', 'depth'), axis=1, tiled=True)  14.1 us
    reshape x1, local copies, waits for them, and re-layouts, laid_out(): return jnp.moveaxis(tiles, 0, dim).reshape(lengths)  12.8 us
    transpose x1, local copies, waits for them, and re-layouts, laid_out(): return jnp.moveaxis(tiles, 0, dim).reshape(lengths)  10.1 us
    dot_general x1, matrix products, per_device(): jnp.einsum('ikc,jkc->ijc', left_all, needed, preferred_element_type=jnp.f...  8.97 us
  transfers between devices with their start and end apart: 5, of which 5 were waited for; matrix products, arithmetic and copies ran while one was open for 6% of the time, Pallas kernels for 0%

commit v1 on v0

v1 whole, which is shorter than its diff:
```python
import functools

import jax
import jax.numpy as jnp
from jax import lax
from jax.experimental import pallas as pl
from jax.experimental.pallas import tpu as pltpu
from jax.sharding import PartitionSpec as P

F32 = jnp.float32
BF16 = jnp.bfloat16
EPS = 1e-05
NT = (((1,), (1,)), ((), ()))
TN = (((0,), (0,)), ((), ()))


def remote(src, dst, send_sem, recv_sem, row, col, depth):
    return pltpu.make_async_remote_copy(
        src_ref=src,
        dst_ref=dst,
        send_sem=send_sem,
        recv_sem=recv_sem,
        device_id=(row, col, depth),
        device_id_type=pl.DeviceIdType.MESH,
    )


def kernel(
    pair,
    ln_gain,
    ln_shift,
    proj_weight,
    proj_bias,
    gate_weight,
    gate_bias,
    out_gain,
    out_shift,
    out_weight,
    out_bias,
    out,
    wt,
    bt,
    normed,
    gate,
    stage,
    sbuf,
    rbuf,
    left,
    ring,
    tsend,
    trecv,
    wide,
    x_send,
    x_recv,
    r_send,
    r_recv,
    t_send,
    t_recv,
    o_send,
    o_recv,
):
    row = lax.axis_index("row")
    x = lax.axis_index("col")
    d = lax.axis_index("depth")
    z = row // 2
    yh = row % 2
    yl = d // 2
    core = d % 2
    me = x * 2 + yh

    barrier = pltpu.get_barrier_semaphore()

    def greet(p, carry):
        prow = z * 2 + p // 16
        pcol = (p // 4) % 4
        pd = p % 4
        other = jnp.logical_or(prow != row, jnp.logical_or(pcol != x, pd != d))

        @pl.when(other)
        def _():
            pl.semaphore_signal(
                barrier, inc=1, device_id=(prow, pcol, pd), device_id_type=pl.DeviceIdType.MESH
            )

        return carry

    lax.fori_loop(0, 32, greet, 0)
    up = (row + 2) % 16
    down = (row + 14) % 16
    for nrow in (up, down):
        pl.semaphore_signal(
            barrier, inc=1, device_id=(nrow, x, d), device_id_type=pl.DeviceIdType.MESH
        )

    for b in range(4):
        wt[b * 128 : (b + 1) * 128, :] = (
            proj_weight[:, b * 128 : (b + 1) * 128].astype(F32).T.astype(BF16)
        )
        bt[b * 128 : (b + 1) * 128, :] = jnp.broadcast_to(
            proj_bias[:, b * 128 : (b + 1) * 128], (128, 128)
        ).T
    first = pl.multiple_of(d * 32, 32)
    wsel = jnp.concatenate([wt[pl.ds(first + 128 * b, 32), :] for b in range(4)], axis=0)
    gain = ln_gain[...]
    shift = ln_shift[...]

    def norm_rows(t, carry):
        vals = jnp.concatenate([pair[t], pair[t + 24]], axis=0).astype(F32)
        centred = vals - jnp.mean(vals, axis=-1, keepdims=True)
        spread = jnp.mean(centred * centred, axis=-1, keepdims=True)
        rows = (centred * lax.rsqrt(spread + EPS) * gain + shift).astype(BF16)
        normed[t] = rows[:192]
        normed[t + 24] = rows[192:]
        mixed = lax.dot_general(wsel, rows, NT, preferred_element_type=F32)
        at = pl.ds(pl.multiple_of(t * 32, 32), 32)
        for q in range(3):
            part = [
                mixed[b * 32 : (b + 1) * 32, q * 128 : (q + 1) * 128]
                + bt[pl.ds(first + 128 * b, 32), :]
                for b in range(4)
            ]
            stage[0, q, at, :] = jax.nn.sigmoid(part[2]) * part[3]
            stage[1, q, at, :] = jax.nn.sigmoid(part[0]) * part[1]
        return carry

    lax.fori_loop(0, 24, norm_rows, 0)
    pl.semaphore_wait(barrier, 33)

    def exchange(kind):
        def body(g, carry):
            for q in range(3):
                rows = [
                    stage[kind, q, pl.ds(g * 4 + c, 24, stride=32), :] for c in range(4)
                ]
                sbuf[kind, g, :, q * 128 : (q + 1) * 128] = jnp.concatenate(rows, axis=0).astype(
                    BF16
                )

            @pl.when(g != me)
            def _():
                remote(
                    sbuf.at[kind, g],
                    rbuf.at[kind, me],
                    x_send.at[kind],
                    x_recv.at[kind],
                    z * 2 + g % 2,
                    g // 2,
                    d,
                ).start()

            @pl.when(g == me)
            def _():
                pltpu.make_async_copy(
                    sbuf.at[kind, g], rbuf.at[kind, me], x_recv.at[kind]
                ).start()

            return carry

        lax.fori_loop(0, 8, body, 0)

    def unpack(kind, put):
        low = lax.broadcasted_iota(jnp.int32, (24, 128), 1) < 64
        for u in range(2):
            for y in range(2):
                one = rbuf[kind, 4 * u + y].astype(F32)
                two = rbuf[kind, 4 * u + 2 + y].astype(F32)
                for c in range(4):
                    a = [one[c * 24 : (c + 1) * 24, q * 128 : (q + 1) * 128] for q in range(3)]
                    b = [two[c * 24 : (c + 1) * 24, q * 128 : (q + 1) * 128] for q in range(3)]
                    ra1 = pltpu.roll(a[1], 64, 1)
                    ra2 = pltpu.roll(a[2], 64, 1)
                    rb0 = pltpu.roll(b[0], 64, 1)
                    rb1 = pltpu.roll(b[1], 64, 1)
                    evens = [a[0], jnp.where(low, a[1], rb0), jnp.where(low, rb0, rb1)]
                    odds = [jnp.where(low, ra1, ra2), jnp.where(low, ra2, b[1]), b[2]]
                    for q in range(3):
                        put(c, u, y, q, jnp.concatenate([evens[q], odds[q]], axis=0).astype(BF16))

    def put_ring(c, u, y, q, tile):
        ring[z, c, u, y * 48 : (y + 1) * 48, q * 128 : (q + 1) * 128] = tile

    def put_left(c, u, y, q, tile):
        left[c, u, y * 48 : (y + 1) * 48, q * 128 : (q + 1) * 128] = tile

    def ring_copy(way, step, c):
        held = (z + 8 - step + 1) % 8 if way == 0 else (z + step - 1) % 8
        piece = ring.at[held, c]
        return remote(
            piece,
            piece,
            r_send.at[way, step - 1, c],
            r_recv.at[way, step - 1, c],
            up if way == 0 else down,
            x,
            d,
        )

    def multiply(plane, c):
        total = lax.dot_general(left[c, 0], ring[plane, c, 0], NT, preferred_element_type=F32)
        total += lax.dot_general(left[c, 1], ring[plane, c, 1], NT, preferred_element_type=F32)
        total = total.astype(BF16)
        tsend[plane * 2, c * 48 : (c + 1) * 48, 0:96] = total[:48]
        tsend[plane * 2 + 1, c * 48 : (c + 1) * 48, 0:96] = total[48:]

    def hand_out(plane):
        pcol = plane // 2
        pcore = plane % 2
        slot = d * 8 + me

        def body(n, carry):
            ph = n // 2
            rel = n % 2
            pl_lo = (yl + rel) % 2
            prow = z * 2 + ph
            pd = pl_lo * 2 + pcore
            other = jnp.logical_or(prow != row, jnp.logical_or(pcol != x, pd != d))

            @pl.when(other)
            def _():
                remote(
                    tsend.at[plane * 2 + ph],
                    trecv.at[slot],
                    t_send.at[rel],
                    t_recv.at[0],
                    prow,
                    pcol,
                    pd,
                ).start()

            @pl.when(jnp.logical_not(other))
            def _():
                pltpu.make_async_copy(
                    tsend.at[plane * 2 + ph], trecv.at[slot], t_recv.at[0]
                ).start()

            return carry

        lax.fori_loop(0, 4, body, 0)

    exchange(0)
    exchange(1)
    tsend[...] = jnp.zeros_like(tsend)

    pltpu.make_async_copy(sbuf.at[0], rbuf.at[0], x_recv.at[0]).wait()
    unpack(0, put_ring)
    for c in range(4):
        ring_copy(0, 1, c).start()
        ring_copy(1, 1, c).start()

    mine = pl.ds(pl.multiple_of(core * 96, 96), 96)

    def gate_rows(i, carry):
        gate[i] = jax.nn.sigmoid(
            jnp.dot(normed[i, mine, :], gate_weight[...], preferred_element_type=F32)
            + gate_bias[...]
        )
        return carry

    lax.fori_loop(0, 48, gate_rows, 0)
    pltpu.make_async_copy(sbuf.at[1], rbuf.at[1], x_recv.at[1]).wait()
    unpack(1, put_left)
    for c in range(4):
        multiply(z, c)
    hand_out(z)

    for step in range(1, 5):
        plus = (z + 8 - step) % 8
        minus = (z + step) % 8
        for c in range(4):
            for way in range(2):
                if step < 4 or c // 2 == way:
                    ring_copy(way, step, c).wait_recv()
                    if step < 3 or (step == 3 and c // 2 == way):
                        ring_copy(way, step + 1, c).start()
            multiply(plus, c)
            if step < 4:
                multiply(minus, c)
        hand_out(plus)
        if step < 4:
            hand_out(minus)

    out_gains = jnp.broadcast_to(out_gain[...], (128, 128)).T
    out_shifts = jnp.broadcast_to(out_shift[...], (128, 128)).T
    wide_copy = pltpu.make_async_copy(trecv, trecv, t_recv.at[0])
    wide_copy.wait()

    def widen(s, carry):
        wide[pl.ds(pl.multiple_of(s * 192, 192), 192), :] = trecv[s].astype(F32)
        return carry

    lax.fori_loop(0, 32, widen, 0)

    def finish_row(i):
        vals = wide[pl.ds(i, 128, stride=48), :]
        centred = vals - jnp.mean(vals, axis=0, keepdims=True)
        spread = jnp.mean(centred * centred, axis=0, keepdims=True)
        rows = (centred * lax.rsqrt(spread + EPS) * out_gains + out_shifts).T.astype(BF16)
        projected = (
            jnp.dot(rows[:96], out_weight[...], preferred_element_type=F32) + out_bias[...]
        )
        out[i, mine, :] = (gate[i] * projected).astype(BF16)

    def swap(n):
        part = out.at[pl.ds(n * 12, 12), mine]
        return remote(part, part, o_send.at[n], o_recv.at[n], row, x, yl * 2 + 1 - core)

    for n in range(4):

        def body(k, carry, n=n):
            finish_row(n * 12 + k)
            return carry

        lax.fori_loop(0, 12, body, 0)
        swap(n).start()

    for kind in range(2):
        pltpu.make_async_copy(
            sbuf.at[kind, pl.ds(0, 7)], rbuf.at[kind, pl.ds(0, 7)], x_send.at[kind]
        ).wait()
    for step in range(1, 5):
        for c in range(4):
            for way in range(2):
                if step < 4 or c // 2 == way:
                    ring_copy(way, step, c).wait_send()
    for rel in range(2):
        units = pl.ds(0, 15 if rel == 0 else 16)
        pltpu.make_async_copy(tsend.at[units], trecv.at[units], t_send.at[rel]).wait()
    for n in range(4):
        swap(n).wait()


def per_device(pair, ln_gain, ln_shift, proj_weight, proj_bias, gate_weight, gate_bias, out_gain, out_shift, out_weight, out_bias):
    line = lambda v: v.reshape(1, -1)
    vmem = pl.BlockSpec(memory_space=pltpu.VMEM)
    dma = pltpu.SemaphoreType.DMA
    return pl.pallas_call(
        kernel,
        out_shape=jax.ShapeDtypeStruct(pair.shape, BF16),
        in_specs=[vmem] * 11,
        out_specs=vmem,
        scratch_shapes=[
            pltpu.VMEM((512, 128), BF16),
            pltpu.VMEM((512, 128), F32),
            pltpu.VMEM((48, 192, 128), BF16),
            pltpu.VMEM((48, 96, 128), F32),
            pltpu.VMEM((2, 3, 24 * 32, 128), F32),
            pltpu.VMEM((2, 8, 96, 384), BF16),
            pltpu.VMEM((2, 8, 96, 384), BF16),
            pltpu.VMEM((4, 2, 96, 384), BF16),
            pltpu.VMEM((8, 4, 2, 96, 384), BF16),
            pltpu.VMEM((16, 192, 128), BF16),
            pltpu.VMEM((32, 192, 128), BF16),
            pltpu.VMEM((6144, 128), F32),
            dma((2,)),
            dma((2,)),
            dma((2, 4, 4)),
            dma((2, 4, 4)),
            dma((2,)),
            dma((1,)),
            dma((4,)),
            dma((4,)),
        ],
        compiler_params=pltpu.CompilerParams(
            collective_id=0, has_side_effects=True, vmem_limit_bytes=56 * 1024 * 1024
        ),
    )(
        pair,
        line(ln_gain),
        line(ln_shift),
        proj_weight,
        line(proj_bias),
        gate_weight,
        line(gate_bias),
        line(out_gain),
        line(out_shift),
        out_weight,
        line(out_bias),
    )


def solution(mesh):
    in_specs = (P("row", "col", None),) + (P(),) * 10
    return jax.shard_map(
        per_device, mesh=mesh, in_specs=in_specs, out_specs=P("row", "col", None), check_vma=False
    )
```

time: 420 us -> 108 us (0.26)
  waiting for transfers between devices: 225 us -> 0 us
  Pallas kernels: 0 us -> 103 us
  blocking collectives: 91.9 us -> 0 us
  local copies, waits for them, and re-layouts: 51.8 us -> 3.22 us
  other arithmetic: 16.3 us -> 0 us
  between operations: 13.3 us -> 0.01 us
  matrix products: 12.3 us -> 0 us
  starting transfers between devices: 8.26 us -> 0 us
    all_gather x4 -> x0, waiting for transfers between devices: 180 us -> none  [the longest x2 136 us: gather_axes(): shard = lax.all_gather(shard, axis, axis=dim, tiled=True)]
    pallas_call x0 -> x1, Pallas kernels: none -> 103 us  [per_device(): pl.pallas_call(kernel, out_shape=jax.ShapeDtypeStruct(pair.shape, BF16),...]
    all_to_all x1 -> x0, blocking collectives: 91.9 us -> none  [cut_exchange(): lax.all_to_all(share, axis, split_axis=0, concat_axis=0, tiled=True)]
    all_to_all x1 -> x0, waiting for transfers between devices: 44.6 us -> none  [cut_exchange(): lax.all_to_all(share, axis, split_axis=0, concat_axis=0, tiled=True)]
    all_gather x1 -> x0, local copies, waits for them, and re-layouts: 14.1 us -> none  [per_device(): left_all = lax.all_gather(left, ('col', 'depth'), axis=1, tiled=True)]
    reshape x2 -> x0, local copies, waits for them, and re-layouts: 13.8 us -> none  [the longest x1 12.8 us: laid_out(): return jnp.moveaxis(tiles, 0, dim).reshape(lengths)]
    dot_general x4 -> x0, matrix products: 12.3 us -> none  [the longest x1 8.97 us: per_device(): jnp.einsum('ikc,jkc->ijc', left_all, needed, preferred_element_type=jnp.f...]
    transpose x1 -> x0, local copies, waits for them, and re-layouts: 10.1 us -> none  [laid_out(): return jnp.moveaxis(tiles, 0, dim).reshape(lengths)]
  transfers between devices with their start and end apart: 5 -> 0, of which waited for: 5 -> 0; matrix products, arithmetic and copies ran while one was open for 6% -> 0% of each run, Pallas kernels for 0% -> 0%
where the time goes in v1:
time: 108 us; the launch traced here: 106 us
  Pallas kernels  103 us (95%)
  local copies, waits for them, and re-layouts  3.22 us (3%)
    pallas_call x1, Pallas kernels, per_device(): pl.pallas_call(kernel, out_shape=jax.ShapeDtypeStruct(pair.shape, BF16),...  103 us
    unnamed x1, local copies, waits for them, and re-layouts  3.22 us

profile of v1, /device:TPU:5, one launch (start us, length us, event | category | flops | bytes accessed | tf_op | source)
XLA Modules:
  0.0 105.8 jit_solution(4477496907201013820)
XLA Ops:
  0.0 102.6 %shard_map.109 = bf16[48,192,128]{2,1,0:T(8,128)(2,1)} custom-call(bf16[48,192,128]{2,1,0:T(8,128)(2,1)} %pair.1, f32[1,128]{1,0:T(1,128)} %bitcast.8, f32[1,128]{1,0:T(1,128)} %bitcast.9, bf16[128,512]{1,0:T(8,128)(2,1)} %proj_weight.1, f32[1,512]{1,0:T(1,128)} %bitcast.7, bf16[128,128]{1,0:T(8,128)(2,1)} %gate_weight.1, f32[1,128]{1,0:T(1,128)} %bitcast.10, ...), custom_call_target="tpu_custom_call" | custom-call | tf_op jit(solution)/shard_map/pallas_call | solution.py:336
  102.6 3.2 %copy.13 = bf16[48,192,128]{2,1,0:T(8,128)(2,1)} copy(bf16[48,192,128]{2,1,0:T(8,128)(2,1)} %shard_map.109) | data formatting | bytes 4718592

commit v2 on v1

v2 whole, which is shorter than its diff:
```python
import functools

import jax
import jax.numpy as jnp
from jax import lax
from jax.experimental import pallas as pl
from jax.experimental.pallas import tpu as pltpu
from jax.sharding import PartitionSpec as P

F32 = jnp.float32
BF16 = jnp.bfloat16
EPS = 1e-05
NT = (((1,), (1,)), ((), ()))
VMEM_MIB = 40


def remote(src, dst, send_sem, recv_sem, row, col, depth):
    return pltpu.make_async_remote_copy(
        src_ref=src,
        dst_ref=dst,
        send_sem=send_sem,
        recv_sem=recv_sem,
        device_id=(row, col, depth),
        device_id_type=pl.DeviceIdType.MESH,
    )


def kernel(
    pair_hbm,
    ln_gain,
    ln_shift,
    proj_weight,
    proj_bias,
    gate_weight,
    gate_bias,
    out_gain,
    out_shift,
    out_weight,
    out_bias,
    out,
    pair,
    wt,
    bt,
    normed,
    gate,
    stage,
    sbuf,
    rbuf,
    left,
    ring,
    tsend,
    trecv,
    wide,
    table,
    p_sem,
    x_send,
    x_recv,
    r_send,
    r_recv,
    h_send,
    h_recv,
    t_send,
    t_recv,
    o_send,
    o_recv,
):
    row = lax.axis_index("row")
    x = lax.axis_index("col")
    d = lax.axis_index("depth")
    z = row // 2
    yh = row % 2
    yl = d // 2
    core = d % 2
    me = x * 2 + yh

    def load(p, half):
        rows = pl.ds(half * 24 + p * 8, 8)
        return pltpu.make_async_copy(pair_hbm.at[rows], pair.at[rows], p_sem.at[p, half])

    for p in range(3):
        for half in range(2):
            load(p, half).start()

    barrier = pltpu.get_barrier_semaphore()

    def greet(p, carry):
        prow = z * 2 + p // 16
        pcol = (p // 4) % 4
        pd = p % 4
        other = jnp.logical_or(prow != row, jnp.logical_or(pcol != x, pd != d))

        @pl.when(other)
        def _():
            pl.semaphore_signal(
                barrier, inc=1, device_id=(prow, pcol, pd), device_id_type=pl.DeviceIdType.MESH
            )

        return carry

    lax.fori_loop(0, 32, greet, 0)
    up = (row + 2) % 16
    down = (row + 14) % 16
    for nrow in (up, down):
        pl.semaphore_signal(
            barrier, inc=1, device_id=(nrow, x, d), device_id_type=pl.DeviceIdType.MESH
        )

    for b in range(4):
        wt[b * 128 : (b + 1) * 128, :] = (
            proj_weight[:, b * 128 : (b + 1) * 128].astype(F32).T.astype(BF16)
        )
        bt[b * 128 : (b + 1) * 128, :] = jnp.broadcast_to(
            proj_bias[:, b * 128 : (b + 1) * 128], (128, 128)
        ).T
    first = pl.multiple_of(d * 32, 32)
    wsel = jnp.concatenate([wt[pl.ds(first + 128 * b, 32), :] for b in range(4)], axis=0)
    gain = ln_gain[...]
    shift = ln_shift[...]

    def project(p):
        def body(n, carry):
            t = p * 8 + n
            vals = jnp.concatenate([pair[t], pair[t + 24]], axis=0).astype(F32)
            centred = vals - jnp.mean(vals, axis=-1, keepdims=True)
            spread = jnp.mean(centred * centred, axis=-1, keepdims=True)
            rows = (centred * lax.rsqrt(spread + EPS) * gain + shift).astype(BF16)
            normed[t] = rows[:192]
            normed[t + 24] = rows[192:]
            mixed = lax.dot_general(wsel, rows, NT, preferred_element_type=F32)
            at = pl.ds(pl.multiple_of(n * 32, 32), 32)
            for q in range(3):
                cut = [
                    mixed[b * 32 : (b + 1) * 32, q * 128 : (q + 1) * 128]
                    + bt[pl.ds(first + 128 * b, 32), :]
                    for b in range(4)
                ]
                stage[0, p, q, at, :] = jax.nn.sigmoid(cut[2]) * cut[3]
                stage[1, p, q, at, :] = jax.nn.sigmoid(cut[0]) * cut[1]
            return carry

        for half in range(2):
            load(p, half).wait()
        lax.fori_loop(0, 8, body, 0, unroll=2)

    def exchange(kind, p):
        def body(g, carry):
            for q in range(3):
                rows = [
                    stage[kind, p, q, pl.ds(g * 4 + c, 8, stride=32), :] for c in range(4)
                ]
                sbuf[kind, p, g, :, q * 128 : (q + 1) * 128] = jnp.concatenate(
                    rows, axis=0
                ).astype(BF16)

            @pl.when(g != me)
            def _():
                remote(
                    sbuf.at[kind, p, g],
                    rbuf.at[kind, p, me],
                    x_send.at[kind, p],
                    x_recv.at[kind, p],
                    z * 2 + g % 2,
                    g // 2,
                    d,
                ).start()

            @pl.when(g == me)
            def _():
                pltpu.make_async_copy(
                    sbuf.at[kind, p, g], rbuf.at[kind, p, me], x_recv.at[kind, p]
                ).start()

            return carry

        lax.fori_loop(0, 8, body, 0)

    low = lax.broadcasted_iota(jnp.int32, (32, 128), 1) < 64

    def unpack(kind, p, put):
        pltpu.make_async_copy(sbuf.at[kind, p], rbuf.at[kind, p], x_recv.at[kind, p]).wait()
        for u in range(2):
            for y in range(2):
                one = rbuf[kind, p, 4 * u + y].astype(F32)
                two = rbuf[kind, p, 4 * u + 2 + y].astype(F32)
                a = [one[:, q * 128 : (q + 1) * 128] for q in range(3)]
                b = [two[:, q * 128 : (q + 1) * 128] for q in range(3)]
                ra1 = pltpu.roll(a[1], 64, 1)
                ra2 = pltpu.roll(a[2], 64, 1)
                rb0 = pltpu.roll(b[0], 64, 1)
                rb1 = pltpu.roll(b[1], 64, 1)
                evens = [a[0], jnp.where(low, a[1], rb0), jnp.where(low, rb0, rb1)]
                odds = [jnp.where(low, ra1, ra2), jnp.where(low, ra2, b[1]), b[2]]
                for c in range(4):
                    at = slice(c * 8, c * 8 + 8)
                    for q in range(3):
                        put(
                            c, u, y, slice(q * 128, q * 128 + 128),
                            jnp.concatenate([evens[q][at], odds[q][at]], axis=0).astype(BF16),
                        )

    def unpack_right(p):
        def put(c, u, y, lanes, tile):
            ring[z, p, c, u, y * 16 : y * 16 + 16, lanes] = tile

        unpack(0, p, put)

    def unpack_left(p):
        def put(c, u, y, lanes, tile):
            left[c, u, p * 32 + y * 16 : p * 32 + y * 16 + 16, lanes] = tile

        unpack(1, p, put)

    def ring_copy(way, step, p):
        held = (z + 8 - step + 1) % 8 if way == 0 else (z + step - 1) % 8
        to = up if way == 0 else down
        if step < 4:
            piece = ring.at[held, p]
            return remote(
                piece, piece, r_send.at[way, step - 1, p], r_recv.at[way, step - 1, p], to, x, d
            )
        piece = ring.at[held, p, pl.ds(way * 2, 2)]
        return remote(piece, piece, h_send.at[way, p], h_recv.at[way, p], to, x, d)

    lane_group = lax.broadcasted_iota(jnp.int32, (96, 128), 1) // 32

    def multiply(plane, p):
        tile = None
        for c in range(4):
            total = None
            for u in range(2):
                rows = ring[plane, p, c, u]
                term = lax.dot_general(
                    left[c, u],
                    jnp.concatenate([rows] * 4, axis=0),
                    NT,
                    preferred_element_type=F32,
                )
                total = term if total is None else total + term
            tile = total if tile is None else jnp.where(lane_group == c, total, tile)
        tile = tile.astype(BF16)
        for ph in range(2):
            tsend[(plane * 3 + p) * 2 + ph] = jnp.concatenate(
                [tile[k * 32 + ph * 16 : k * 32 + ph * 16 + 16] for k in range(3)], axis=0
            )
        hand_out(plane, p)

    def hand_out(plane, p):
        pcol = plane // 2
        pcore = plane % 2
        slot = d * 8 + me
        for ph in range(2):
            for rel in range(2):
                prow = z * 2 + ph
                pd = ((yl + rel) % 2) * 2 + pcore
                unit = tsend.at[(plane * 3 + p) * 2 + ph]
                copy = remote(
                    unit, trecv.at[p, slot], t_send.at[rel], t_recv.at[p], prow, pcol, pd
                )
                if rel == 1:
                    copy.start()
                    continue
                other = jnp.logical_or(prow != row, jnp.logical_or(pcol != x, pd != d))

                @pl.when(other)
                def _():
                    copy.start()

                @pl.when(jnp.logical_not(other))
                def _():
                    pltpu.make_async_copy(unit, trecv.at[p, slot], t_recv.at[p]).start()

    def start_ring(p):
        unpack_right(p)
        ring_copy(0, 1, p).start()
        ring_copy(1, 1, p).start()

    project(0)
    pl.semaphore_wait(barrier, 33)
    exchange(0, 0)
    project(1)
    exchange(0, 1)
    start_ring(0)
    project(2)
    exchange(0, 2)
    start_ring(1)
    for p in range(3):
        exchange(1, p)
    start_ring(2)

    mine = pl.ds(pl.multiple_of(core * 96, 96), 96)

    def gate_rows(n, carry):
        at = pl.ds(n * 4, 4)
        logits = (
            jnp.dot(
                normed[at, mine, :].reshape(384, 128),
                gate_weight[...],
                preferred_element_type=F32,
            )
            + gate_bias[...]
        )
        gate[at] = jax.nn.sigmoid(logits).reshape(4, 96, 128)
        return carry

    lax.fori_loop(0, 12, gate_rows, 0)
    table[0] = jnp.broadcast_to(out_gain[...], (128, 128)).T
    table[1] = jnp.broadcast_to(out_shift[...], (128, 128)).T
    table[2] = out_weight[...].astype(F32)

    for p in range(3):
        unpack_left(p)

    for step in range(1, 5):
        plus = (z + 8 - step) % 8
        minus = (z + step) % 8
        for p in range(3):
            for way in range(2):
                ring_copy(way, step, p).wait_recv()
                if step < 4:
                    ring_copy(way, step + 1, p).start()
            if step == 1:
                multiply(z, p)
            multiply(plus, p)
            if step < 4:
                multiply(minus, p)

    def regroup(n):
        return jnp.concatenate(
            [table[n, pl.ds(c, 32, stride=4), :] for c in range(4)], axis=0
        )

    gains = regroup(0)
    shifts = regroup(1)
    weight = regroup(2).astype(BF16)
    group = lax.broadcasted_iota(jnp.int32, (32, 128), 1) // 32

    def swap(p, k):
        part = out.at[:, pl.ds(pl.multiple_of(core * 96 + k * 24 + p * 8, 8), 8), :]
        return remote(
            part, part, o_send.at[p, k], o_recv.at[p, k], row, x, yl * 2 + 1 - core
        )

    for p in range(3):
        pltpu.make_async_copy(trecv.at[p], trecv.at[p], t_recv.at[p]).wait()

        def widen(s, carry, p=p):
            at = pl.ds(pl.multiple_of(s * 192, 192), 192)
            wide[at, :] = trecv[p, pl.ds(s * 4, 4)].reshape(192, 128).astype(F32)
            return carry

        lax.fori_loop(0, 8, widen, 0, unroll=2)

        def finish(g, carry, p=p):
            from_row = [wide[pl.ds(g * 4 + i, 32, stride=48), :] for i in range(4)]
            blocks = []
            for c in range(4):
                block = None
                for i in range(4):
                    turn = (32 * (i - c)) % 128
                    moved = pltpu.roll(from_row[i], turn, 1) if turn else from_row[i]
                    block = moved if block is None else jnp.where(group == i, moved, block)
                blocks.append(block)
            vals = jnp.concatenate(blocks, axis=0)
            centred = vals - jnp.mean(vals, axis=0, keepdims=True)
            spread = jnp.mean(centred * centred, axis=0, keepdims=True)
            rows = (centred * lax.rsqrt(spread + EPS) * gains + shifts).T.astype(BF16)
            projected = jnp.dot(rows, weight, preferred_element_type=F32) + out_bias[...]
            for i in range(4):
                line = ((g % 4) // 2) * 24 + (g // 4) * 8 + (g % 2) * 4 + i
                for k in range(4):
                    j = k * 24 + p * 8
                    value = (
                        gate[line, j : j + 8, :]
                        * projected[i * 32 + k * 8 : i * 32 + k * 8 + 8]
                    )
                    out[line, pl.ds(pl.multiple_of(core * 96 + j, 8), 8), :] = value.astype(BF16)
            return carry

        lax.fori_loop(0, 12, finish, 0, unroll=2)
        for k in range(4):
            swap(p, k).start()

    for kind in range(2):
        for p in range(3):
            pltpu.make_async_copy(
                sbuf.at[kind, p, pl.ds(0, 7)], rbuf.at[kind, p, pl.ds(0, 7)], x_send.at[kind, p]
            ).wait()
    for step in range(1, 5):
        for p in range(3):
            for way in range(2):
                ring_copy(way, step, p).wait_send()
    for rel in range(2):
        units = tsend.at[pl.ds(0, 45 if rel == 0 else 48)]
        pltpu.make_async_copy(units, units, t_send.at[rel]).wait()
    for p in range(3):
        for k in range(4):
            swap(p, k).wait()


def per_device(
    pair,
    ln_gain,
    ln_shift,
    proj_weight,
    proj_bias,
    gate_weight,
    gate_bias,
    out_gain,
    out_shift,
    out_weight,
    out_bias,
):
    line = lambda v: v.reshape(1, -1)
    vmem = pl.BlockSpec(memory_space=pltpu.VMEM)
    dma = pltpu.SemaphoreType.DMA
    return pl.pallas_call(
        kernel,
        out_shape=jax.ShapeDtypeStruct(pair.shape, BF16),
        in_specs=[pl.BlockSpec(memory_space=pl.ANY)] + [vmem] * 10,
        out_specs=vmem,
        scratch_shapes=[
            pltpu.VMEM((48, 192, 128), BF16),
            pltpu.VMEM((512, 128), BF16),
            pltpu.VMEM((512, 128), F32),
            pltpu.VMEM((48, 192, 128), BF16),
            pltpu.VMEM((48, 96, 128), F32),
            pltpu.VMEM((2, 3, 3, 256, 128), F32),
            pltpu.VMEM((2, 3, 8, 32, 384), BF16),
            pltpu.VMEM((2, 3, 8, 32, 384), BF16),
            pltpu.VMEM((4, 2, 96, 384), BF16),
            pltpu.VMEM((8, 3, 4, 2, 32, 384), BF16),
            pltpu.VMEM((48, 48, 128), BF16),
            pltpu.VMEM((3, 32, 48, 128), BF16),
            pltpu.VMEM((1536, 128), F32),
            pltpu.VMEM((3, 128, 128), F32),
            dma((3, 2)),
            dma((2, 3)),
            dma((2, 3)),
            dma((2, 3, 3)),
            dma((2, 3, 3)),
            dma((2, 3)),
            dma((2, 3)),
            dma((2,)),
            dma((3,)),
            dma((3, 4)),
            dma((3, 4)),
        ],
        compiler_params=pltpu.CompilerParams(
            collective_id=0, has_side_effects=True, vmem_limit_bytes=VMEM_MIB * 1024 * 1024
        ),
    )(
        pair,
        line(ln_gain),
        line(ln_shift),
        proj_weight,
        line(proj_bias),
        gate_weight,
        line(gate_bias),
        line(out_gain),
        line(out_shift),
        out_weight,
        line(out_bias),
    )


def solution(mesh):
    in_specs = (P("row", "col", None),) + (P(),) * 10
    return jax.shard_map(
        per_device, mesh=mesh, in_specs=in_specs, out_specs=P("row", "col", None), check_vma=False
    )
```

time: 108 us -> 87.3 us (0.81); the launches traced: 106 us -> 86.9 us
  Pallas kernels: 103 us -> 76.8 us
  local copies, waits for them, and re-layouts: 3.22 us -> 10.1 us
    pallas_call x1, Pallas kernels: 103 us -> 76.8 us  [per_device(): pl.pallas_call(kernel, out_shape=jax.ShapeDtypeStruct(pair.shape, BF16),...]
    unnamed x1 -> x23, local copies, waits for them, and re-layouts: 3.22 us -> 10.1 us
where the time goes in v2:
time: 87.3 us; the launch traced here: 86.9 us
  Pallas kernels  76.8 us (88%)
  local copies, waits for them, and re-layouts  10.1 us (12%)
    pallas_call x1, Pallas kernels, per_device(): pl.pallas_call(kernel, out_shape=jax.ShapeDtypeStruct(pair.shape, BF16),...  76.8 us
    unnamed x23, local copies, waits for them, and re-layouts  10.1 us

profile of v2, /device:TPU:5, one launch (start us, length us, event | category | flops | bytes accessed | tf_op | source)
XLA Modules:
  0.0 86.9 jit_solution(9922522729713662534)
XLA Ops:
  0.0 0.0 copy-start
  0.0 1.7 %copy-done = bf16[48,192,128]{2,1,0:T(8,128)(2,1)S(1)} copy-done((bf16[48,192,128]{2,1,0:T(8,128)(2,1)S(1)}, bf16[48,192,128]{2,1,0:T(8,128)(2,1)}, u32[]{:S(2)}) %copy-start) | copy-done | bytes 2359320
  1.7 0.0 copy-start.1
  1.7 0.9 %copy-done.1 = bf16[128,512]{1,0:T(8,128)(2,1)S(1)} copy-done((bf16[128,512]{1,0:T(8,128)(2,1)S(1)}, bf16[128,512]{1,0:T(8,128)(2,1)}, u32[]{:S(2)}) %copy-start.1) | copy-done | bytes 131096
  2.6 0.0 copy-start.2
  2.6 0.8 copy-done.2
  3.3 0.0 copy-start.3
  3.3 0.8 copy-done.3
  4.1 0.0 copy-start.4
  4.1 0.7 copy-done.4
  4.8 0.0 copy-start.5
  4.8 0.7 copy-done.5
  5.4 0.0 copy-start.6
  5.4 0.7 copy-done.6
  6.1 0.0 copy-start.7
  6.1 0.7 copy-done.7
  6.7 0.0 copy-start.8
  6.7 0.7 copy-done.8
  7.4 0.0 copy-start.9
  7.4 0.7 copy-done.9
  8.0 0.0 copy-start.10
  8.1 0.7 copy-done.10
  8.7 76.8 %shard_map.109 = bf16[48,192,128]{2,1,0:T(8,128)(2,1)S(1)} custom-call(bf16[48,192,128]{2,1,0:T(8,128)(2,1)S(1)} %copy-done, f32[1,128]{1,0:T(1,128)S(1)} %bitcast.8, f32[1,128]{1,0:T(1,128)S(1)} %bitcast.9, bf16[128,512]{1,0:T(8,128)(2,1)S(1)} %copy-done.1, f32[1,512]{1,0:T(1,128)S(1)} %bitcast.7, bf16[128,128]{1,0:T(8,128)(2,1)S(1)} %copy-done.2, ...), custom_call_target="tpu_custom_call" | custom-call | tf_op jit(solution)/shard_map/pallas_call | solution.py:416
  85.5 1.4 %copy.13 = bf16[48,192,128]{2,1,0:T(8,128)(2,1)} copy(bf16[48,192,128]{2,1,0:T(8,128)(2,1)S(1)} %shard_map.109) | data formatting | bytes 4718592
Async XLA Ops:
  0.0 1.7 %copy-start = (bf16[48,192,128]{2,1,0:T(8,128)(2,1)S(1)}, bf16[48,192,128]{2,1,0:T(8,128)(2,1)}, u32[]{:S(2)}) copy-start(bf16[48,192,128]{2,1,0:T(8,128)(2,1)} %pair_hbm.1) | copy-start | bytes 7077892
  1.7 0.9 %copy-start.1 = (bf16[128,512]{1,0:T(8,128)(2,1)S(1)}, bf16[128,512]{1,0:T(8,128)(2,1)}, u32[]{:S(2)}) copy-start(bf16[128,512]{1,0:T(8,128)(2,1)} %proj_weight.1) | copy-start | bytes 393220
  2.6 0.8 copy-start.2
  3.3 0.8 copy-start.3
  4.1 0.7 copy-start.4
  4.8 0.7 copy-start.5
  5.4 0.7 copy-start.6
  6.1 0.7 copy-start.7
  6.7 0.7 copy-start.8
  7.4 0.7 copy-start.9
  8.0 0.7 copy-start.10

commit v3 on v2

--- a/solution.py
+++ b/solution.py
@@ -11,7 +11,8 @@
 BF16 = jnp.bfloat16
 EPS = 1e-05
 NT = (((1,), (1,)), ((), ()))
-VMEM_MIB = 40
+VMEM_MIB = 50
+UNROLL = 4
 
 
 def remote(src, dst, send_sem, recv_sem, row, col, depth):
@@ -25,8 +26,15 @@
     )
 
 
-def kernel(
+def kernel(*refs):
+    work(refs[0], refs[1:11], refs[12:22], refs[11], *refs[12:])
+
+
+def work(
     pair_hbm,
+    sources,
+    params,
+    out,
     ln_gain,
     ln_shift,
     proj_weight,
@@ -37,7 +45,6 @@
     out_shift,
     out_weight,
     out_bias,
-    out,
     pair,
     wt,
     bt,
@@ -52,6 +59,8 @@
     trecv,
     wide,
     table,
+    normal,
+    w_sem,
     p_sem,
     x_send,
     x_recv,
@@ -77,7 +86,15 @@
         rows = pl.ds(half * 24 + p * 8, 8)
         return pltpu.make_async_copy(pair_hbm.at[rows], pair.at[rows], p_sem.at[p, half])
 
-    for p in range(3):
+    for half in range(2):
+        load(0, half).start()
+    fetches = [
+        pltpu.make_async_copy(src, dst, w_sem.at[n])
+        for n, (src, dst) in enumerate(zip(sources, params))
+    ]
+    for fetch in fetches:
+        fetch.start()
+    for p in range(1, 3):
         for half in range(2):
             load(p, half).start()
 
@@ -104,6 +121,9 @@
         pl.semaphore_signal(
             barrier, inc=1, device_id=(nrow, x, d), device_id_type=pl.DeviceIdType.MESH
         )
+
+    for fetch in fetches:
+        fetch.wait()
 
     for b in range(4):
         wt[b * 128 : (b + 1) * 128, :] = (
@@ -279,9 +299,9 @@
     exchange(0, 0)
     project(1)
     exchange(0, 1)
-    start_ring(0)
     project(2)
     exchange(0, 2)
+    start_ring(0)
     start_ring(1)
     for p in range(3):
         exchange(1, p)
@@ -363,10 +383,17 @@
             vals = jnp.concatenate(blocks, axis=0)
             centred = vals - jnp.mean(vals, axis=0, keepdims=True)
             spread = jnp.mean(centred * centred, axis=0, keepdims=True)
-            rows = (centred * lax.rsqrt(spread + EPS) * gains + shifts).T.astype(BF16)
+            rows = (centred * lax.rsqrt(spread + EPS) * gains + shifts).astype(BF16)
+            normal[pl.ds(pl.multiple_of(g * 128, 128), 128), :] = rows.T
+            return carry
+
+        lax.fori_loop(0, 12, finish, 0, unroll=UNROLL)
+
+        def apply(g, carry, p=p):
+            rows = normal[pl.ds(pl.multiple_of(g * 256, 256), 256), :]
             projected = jnp.dot(rows, weight, preferred_element_type=F32) + out_bias[...]
-            for i in range(4):
-                line = ((g % 4) // 2) * 24 + (g // 4) * 8 + (g % 2) * 4 + i
+            for i in range(8):
+                line = (g % 2) * 24 + (g // 2) * 8 + i
                 for k in range(4):
                     j = k * 24 + p * 8
                     value = (
@@ -376,7 +403,7 @@
                     out[line, pl.ds(pl.multiple_of(core * 96 + j, 8), 8), :] = value.astype(BF16)
             return carry
 
-        lax.fori_loop(0, 12, finish, 0, unroll=2)
+        lax.fori_loop(0, 6, apply, 0, unroll=2)
         for k in range(4):
             swap(p, k).start()
 
@@ -411,14 +438,28 @@
     out_bias,
 ):
     line = lambda v: v.reshape(1, -1)
+    operands = (
+        pair,
+        line(ln_gain),
+        line(ln_shift),
+        proj_weight,
+        line(proj_bias),
+        gate_weight,
+        line(gate_bias),
+        line(out_gain),
+        line(out_shift),
+        out_weight,
+        line(out_bias),
+    )
     vmem = pl.BlockSpec(memory_space=pltpu.VMEM)
     dma = pltpu.SemaphoreType.DMA
     return pl.pallas_call(
         kernel,
         out_shape=jax.ShapeDtypeStruct(pair.shape, BF16),
-        in_specs=[pl.BlockSpec(memory_space=pl.ANY)] + [vmem] * 10,
+        in_specs=[pl.BlockSpec(memory_space=pl.ANY)] * 11,
         out_specs=vmem,
         scratch_shapes=[
+            *[pltpu.VMEM(v.shape, v.dtype) for v in operands[1:]],
             pltpu.VMEM((48, 192, 128), BF16),
             pltpu.VMEM((512, 128), BF16),
             pltpu.VMEM((512, 128), F32),
@@ -433,6 +474,8 @@
             pltpu.VMEM((3, 32, 48, 128), BF16),
             pltpu.VMEM((1536, 128), F32),
             pltpu.VMEM((3, 128, 128), F32),
+            pltpu.VMEM((1536, 128), BF16),
+            dma((10,)),
             dma((3, 2)),
             dma((2, 3)),
             dma((2, 3)),
@@ -448,19 +491,7 @@
         compiler_params=pltpu.CompilerParams(
             collective_id=0, has_side_effects=True, vmem_limit_bytes=VMEM_MIB * 1024 * 1024
         ),
-    )(
-        pair,
-        line(ln_gain),
-        line(ln_shift),
-        proj_weight,
-        line(proj_bias),
-        gate_weight,
-        line(gate_bias),
-        line(out_gain),
-        line(out_shift),
-        out_weight,
-        line(out_bias),
-    )
+    )(*[pltpu.with_memory_space_constraint(v, pltpu.HBM) for v in operands])
 
 
 def solution(mesh):

time: 87.3 us -> 74.4 us (0.85)
  local copies, waits for them, and re-layouts: 10.1 us -> 1.41 us
  Pallas kernels: 76.8 us -> 72.9 us
    unnamed x23 -> x1, local copies, waits for them, and re-layouts: 10.1 us -> 1.41 us
    pallas_call x1, Pallas kernels: 76.8 us -> 72.9 us  [per_device(): pl.pallas_call(kernel, out_shape=jax.ShapeDtypeStruct(pair.shape, BF16),...]
where the time goes in v3:
time: 74.4 us; the launch traced here: 74.3 us
  Pallas kernels  72.9 us (98%)
  local copies, waits for them, and re-layouts  1.41 us (2%)
    pallas_call x1, Pallas kernels, per_device(): pl.pallas_call(kernel, out_shape=jax.ShapeDtypeStruct(pair.shape, BF16),...  72.9 us

profile of v3, /device:TPU:5, one launch (start us, length us, event | category | flops | bytes accessed | tf_op | source)
XLA Modules:
  0.0 74.3 jit_solution(12308298888742226618)
XLA Ops:
  0.0 72.9 %shard_map.109 = bf16[48,192,128]{2,1,0:T(8,128)(2,1)S(1)} custom-call(bf16[48,192,128]{2,1,0:T(8,128)(2,1)} %refs_0_.1, f32[1,128]{1,0:T(1,128)} %bitcast.8, f32[1,128]{1,0:T(1,128)} %bitcast.9, bf16[128,512]{1,0:T(8,128)(2,1)} %refs_3_.1, f32[1,512]{1,0:T(1,128)} %bitcast.7, bf16[128,128]{1,0:T(8,128)(2,1)} %refs_5_.1, f32[1,128]{1,0:T(1,128)} %bitcast.10, ...), custom_call_target="tpu_custom_call" | custom-call | tf_op jit(solution)/shard_map/pallas_call | solution.py:456
  72.9 1.4 %copy.13 = bf16[48,192,128]{2,1,0:T(8,128)(2,1)} copy(bf16[48,192,128]{2,1,0:T(8,128)(2,1)S(1)} %shard_map.109) | data formatting | bytes 4718592

commit v4 on v3

--- a/solution.py
+++ b/solution.py
@@ -12,7 +12,8 @@
 EPS = 1e-05
 NT = (((1,), (1,)), ((), ()))
 VMEM_MIB = 50
-UNROLL = 4
+UNROLL = 6
+ORDER = (1, 2, 0)
 
 
 def remote(src, dst, send_sem, recv_sem, row, col, depth):
@@ -60,8 +61,14 @@
     wide,
     table,
     normal,
+    raw,
+    raw_in,
     w_sem,
     p_sem,
+    w_send,
+    w_recv,
+    v_send,
+    v_recv,
     x_send,
     x_recv,
     r_send,
@@ -162,7 +169,7 @@
             load(p, half).wait()
         lax.fori_loop(0, 8, body, 0, unroll=2)
 
-    def exchange(kind, p):
+    def pack(kind, p):
         def body(g, carry):
             for q in range(3):
                 rows = [
@@ -171,37 +178,45 @@
                 sbuf[kind, p, g, :, q * 128 : (q + 1) * 128] = jnp.concatenate(
                     rows, axis=0
                 ).astype(BF16)
-
+            return carry
+
+        lax.fori_loop(0, 8, body, 0, unroll=2)
+
+    def spread(source, target, send_sem, recv_sem):
+        def body(g, carry):
             @pl.when(g != me)
             def _():
                 remote(
-                    sbuf.at[kind, p, g],
-                    rbuf.at[kind, p, me],
-                    x_send.at[kind, p],
-                    x_recv.at[kind, p],
-                    z * 2 + g % 2,
-                    g // 2,
-                    d,
+                    source.at[g], target.at[me], send_sem, recv_sem, z * 2 + g % 2, g // 2, d
                 ).start()
 
             @pl.when(g == me)
             def _():
-                pltpu.make_async_copy(
-                    sbuf.at[kind, p, g], rbuf.at[kind, p, me], x_recv.at[kind, p]
-                ).start()
+                pltpu.make_async_copy(source.at[g], target.at[me], recv_sem).start()
 
             return carry
 
         lax.fori_loop(0, 8, body, 0)
 
+    def exchange(kind, p):
+        spread(sbuf.at[kind, p], rbuf.at[kind, p], x_send.at[kind, p], x_recv.at[kind, p])
+
+    def raw_copy(way):
+        to = up if way == 0 else down
+        return remote(sbuf.at[0, 0], raw.at[way], w_send.at[way], w_recv.at[way], to, x, d)
+
+    def raw_spread(way):
+        raw_copy(way).wait_recv()
+        spread(raw.at[way], raw_in.at[way], v_send.at[way], v_recv.at[way])
+
     low = lax.broadcasted_iota(jnp.int32, (32, 128), 1) < 64
 
-    def unpack(kind, p, put):
-        pltpu.make_async_copy(sbuf.at[kind, p], rbuf.at[kind, p], x_recv.at[kind, p]).wait()
+    def unpack(source, recv_sem, put):
+        pltpu.make_async_copy(source, source, recv_sem).wait()
         for u in range(2):
             for y in range(2):
-                one = rbuf[kind, p, 4 * u + y].astype(F32)
-                two = rbuf[kind, p, 4 * u + 2 + y].astype(F32)
+                one = source[4 * u + y].astype(F32)
+                two = source[4 * u + 2 + y].astype(F32)
                 a = [one[:, q * 128 : (q + 1) * 128] for q in range(3)]
                 b = [two[:, q * 128 : (q + 1) * 128] for q in range(3)]
                 ra1 = pltpu.roll(a[1], 64, 1)
@@ -222,13 +237,21 @@
         def put(c, u, y, lanes, tile):
             ring[z, p, c, u, y * 16 : y * 16 + 16, lanes] = tile
 
-        unpack(0, p, put)
+        unpack(rbuf.at[0, p], x_recv.at[0, p], put)
+
+    def unpack_raw(way):
+        plane = (z + 7) % 8 if way == 0 else (z + 1) % 8
+
+        def put(c, u, y, lanes, tile):
+            ring[plane, 0, c, u, y * 16 : y * 16 + 16, lanes] = tile
+
+        unpack(raw_in.at[way], v_recv.at[way], put)
 
     def unpack_left(p):
         def put(c, u, y, lanes, tile):
             left[c, u, p * 32 + y * 16 : p * 32 + y * 16 + 16, lanes] = tile
 
-        unpack(1, p, put)
+        unpack(rbuf.at[1, p], x_recv.at[1, p], put)
 
     def ring_copy(way, step, p):
         held = (z + 8 - step + 1) % 8 if way == 0 else (z + step - 1) % 8
@@ -290,22 +313,32 @@
                     pltpu.make_async_copy(unit, trecv.at[p, slot], t_recv.at[p]).start()
 
     def start_ring(p):
-        unpack_right(p)
         ring_copy(0, 1, p).start()
         ring_copy(1, 1, p).start()
 
     project(0)
+    pack(0, 0)
+    project(1)
+    pack(0, 1)
     pl.semaphore_wait(barrier, 33)
     exchange(0, 0)
-    project(1)
+    raw_copy(0).start()
+    raw_copy(1).start()
     exchange(0, 1)
     project(2)
+    pack(0, 2)
     exchange(0, 2)
-    start_ring(0)
+    for p in range(3):
+        pack(1, p)
+    unpack_right(1)
     start_ring(1)
+    raw_spread(0)
+    raw_spread(1)
+    unpack_right(2)
+    start_ring(2)
     for p in range(3):
         exchange(1, p)
-    start_ring(2)
+    unpack_right(0)
 
     mine = pl.ds(pl.multiple_of(core * 96, 96), 96)
 
@@ -327,21 +360,27 @@
     table[1] = jnp.broadcast_to(out_shift[...], (128, 128)).T
     table[2] = out_weight[...].astype(F32)
 
-    for p in range(3):
-        unpack_left(p)
-
     for step in range(1, 5):
         plus = (z + 8 - step) % 8
         minus = (z + step) % 8
-        for p in range(3):
+        for p in ORDER:
             for way in range(2):
-                ring_copy(way, step, p).wait_recv()
+                if step == 1 and p == 0:
+                    unpack_raw(way)
+                else:
+                    ring_copy(way, step, p).wait_recv()
                 if step < 4:
                     ring_copy(way, step + 1, p).start()
-            if step == 1:
+            if step > 1:
+                multiply(plus, p)
+                if step < 4:
+                    multiply(minus, p)
+        if step == 1:
+            for p in range(3):
+                unpack_left(p)
+            for p in range(3):
                 multiply(z, p)
-            multiply(plus, p)
-            if step < 4:
+                multiply(plus, p)
                 multiply(minus, p)
 
     def regroup(n):
@@ -360,7 +399,7 @@
             part, part, o_send.at[p, k], o_recv.at[p, k], row, x, yl * 2 + 1 - core
         )
 
-    for p in range(3):
+    for p in ORDER:
         pltpu.make_async_copy(trecv.at[p], trecv.at[p], t_recv.at[p]).wait()
 
         def widen(s, carry, p=p):
@@ -412,10 +451,16 @@
             pltpu.make_async_copy(
                 sbuf.at[kind, p, pl.ds(0, 7)], rbuf.at[kind, p, pl.ds(0, 7)], x_send.at[kind, p]
             ).wait()
+    for way in range(2):
+        raw_copy(way).wait_send()
+        pltpu.make_async_copy(
+            raw.at[way, pl.ds(0, 7)], raw_in.at[way, pl.ds(0, 7)], v_send.at[way]
+        ).wait()
     for step in range(1, 5):
         for p in range(3):
             for way in range(2):
-                ring_copy(way, step, p).wait_send()
+                if step > 1 or p > 0:
+                    ring_copy(way, step, p).wait_send()
     for rel in range(2):
         units = tsend.at[pl.ds(0, 45 if rel == 0 else 48)]
         pltpu.make_async_copy(units, units, t_send.at[rel]).wait()
@@ -475,8 +520,14 @@
             pltpu.VMEM((1536, 128), F32),
             pltpu.VMEM((3, 128, 128), F32),
             pltpu.VMEM((1536, 128), BF16),
+            pltpu.VMEM((2, 8, 32, 384), BF16),
+            pltpu.VMEM((2, 8, 32, 384), BF16),
             dma((10,)),
             dma((3, 2)),
+            dma((2,)),
+            dma((2,)),
+            dma((2,)),
+            dma((2,)),
             dma((2, 3)),
             dma((2, 3)),
             dma((2, 3, 3)),

time: 74.4 us -> 73.2 us (0.984)
  Pallas kernels: 72.9 us -> 71.7 us
    pallas_call x1, Pallas kernels: 72.9 us -> 71.7 us  [per_device(): pl.pallas_call(kernel, out_shape=jax.ShapeDtypeStruct(pair.shape, BF16),...]
where the time goes in v4:
time: 73.2 us; the launch traced here: 73.1 us
  Pallas kernels  71.7 us (98%)
  local copies, waits for them, and re-layouts  1.41 us (2%)
    pallas_call x1, Pallas kernels, per_device(): pl.pallas_call(kernel, out_shape=jax.ShapeDtypeStruct(pair.shape, BF16),...  71.7 us

profile of v4, /device:TPU:5, one launch (start us, length us, event | category | flops | bytes accessed | tf_op | source)
XLA Modules:
  0.0 73.1 jit_solution(4339510318014739068)
XLA Ops:
  0.0 71.7 %shard_map.109 = bf16[48,192,128]{2,1,0:T(8,128)(2,1)S(1)} custom-call(bf16[48,192,128]{2,1,0:T(8,128)(2,1)} %refs_0_.1, f32[1,128]{1,0:T(1,128)} %bitcast.8, f32[1,128]{1,0:T(1,128)} %bitcast.9, bf16[128,512]{1,0:T(8,128)(2,1)} %refs_3_.1, f32[1,512]{1,0:T(1,128)} %bitcast.7, bf16[128,128]{1,0:T(8,128)(2,1)} %refs_5_.1, f32[1,128]{1,0:T(1,128)} %bitcast.10, ...), custom_call_target="tpu_custom_call" | custom-call | tf_op jit(solution)/shard_map/pallas_call | solution.py:501
  71.7 1.4 %copy.13 = bf16[48,192,128]{2,1,0:T(8,128)(2,1)} copy(bf16[48,192,128]{2,1,0:T(8,128)(2,1)S(1)} %shard_map.109) | data formatting | bytes 4718592

commit v5 on v4

--- a/solution.py
+++ b/solution.py
@@ -107,26 +107,18 @@
 
     barrier = pltpu.get_barrier_semaphore()
 
-    def greet(p, carry):
-        prow = z * 2 + p // 16
-        pcol = (p // 4) % 4
-        pd = p % 4
-        other = jnp.logical_or(prow != row, jnp.logical_or(pcol != x, pd != d))
-
-        @pl.when(other)
-        def _():
-            pl.semaphore_signal(
-                barrier, inc=1, device_id=(prow, pcol, pd), device_id_type=pl.DeviceIdType.MESH
-            )
-
-        return carry
-
-    lax.fori_loop(0, 32, greet, 0)
     up = (row + 2) % 16
     down = (row + 14) % 16
-    for nrow in (up, down):
+    greeted = [
+        (z * 2 + (yh + a) % 2, (x + b) % 4, (d + e) % 4)
+        for b in (2, 1, 3, 0)
+        for a in (1, 0)
+        for e in (2, 1, 3, 0)
+        if a or b or e
+    ]
+    for device in greeted + [(up, x, d), (down, x, d)]:
         pl.semaphore_signal(
-            barrier, inc=1, device_id=(nrow, x, d), device_id_type=pl.DeviceIdType.MESH
+            barrier, inc=1, device_id=device, device_id_type=pl.DeviceIdType.MESH
         )
 
     for fetch in fetches:
@@ -183,20 +175,12 @@
         lax.fori_loop(0, 8, body, 0, unroll=2)
 
     def spread(source, target, send_sem, recv_sem):
-        def body(g, carry):
-            @pl.when(g != me)
-            def _():
-                remote(
-                    source.at[g], target.at[me], send_sem, recv_sem, z * 2 + g % 2, g // 2, d
-                ).start()
-
-            @pl.when(g == me)
-            def _():
-                pltpu.make_async_copy(source.at[g], target.at[me], recv_sem).start()
-
-            return carry
-
-        lax.fori_loop(0, 8, body, 0)
+        for n in (5, 4, 3, 1, 2, 6, 7):
+            g = (me + n) % 8
+            remote(
+                source.at[g], target.at[me], send_sem, recv_sem, z * 2 + g % 2, g // 2, d
+            ).start()
+        pltpu.make_async_copy(source.at[me], target.at[me], recv_sem).start()
 
     def exchange(kind, p):
         spread(sbuf.at[kind, p], rbuf.at[kind, p], x_send.at[kind, p], x_recv.at[kind, p])
@@ -321,7 +305,6 @@
     project(1)
     pack(0, 1)
     pl.semaphore_wait(barrier, 33)
-    exchange(0, 0)
     raw_copy(0).start()
     raw_copy(1).start()
     exchange(0, 1)
@@ -336,9 +319,9 @@
     raw_spread(1)
     unpack_right(2)
     start_ring(2)
+    exchange(0, 0)
     for p in range(3):
         exchange(1, p)
-    unpack_right(0)
 
     mine = pl.ds(pl.multiple_of(core * 96, 96), 96)
 
@@ -376,6 +359,7 @@
                 if step < 4:
                     multiply(minus, p)
         if step == 1:
+            unpack_right(0)
             for p in range(3):
                 unpack_left(p)
             for p in range(3):
@@ -399,7 +383,29 @@
             part, part, o_send.at[p, k], o_recv.at[p, k], row, x, yl * 2 + 1 - core
         )
 
+    def drain():
+        for kind in range(2):
+            for p in range(3):
+                pltpu.make_async_copy(
+                    sbuf.at[kind, p, pl.ds(0, 7)], rbuf.at[kind, p, pl.ds(0, 7)], x_send.at[kind, p]
+                ).wait()
+        for way in range(2):
+            raw_copy(way).wait_send()
+            pltpu.make_async_copy(
+                raw.at[way, pl.ds(0, 7)], raw_in.at[way, pl.ds(0, 7)], v_send.at[way]
+            ).wait()
+        for step in range(1, 5):
+            for p in range(3):
+                for way in range(2):
+                    if step > 1 or p > 0:
+                        ring_copy(way, step, p).wait_send()
+        for rel in range(2):
+            units = tsend.at[pl.ds(0, 45 if rel == 0 else 48)]
+            pltpu.make_async_copy(units, units, t_send.at[rel]).wait()
+
     for p in ORDER:
+        if p == ORDER[2]:
+            drain()
         pltpu.make_async_copy(trecv.at[p], trecv.at[p], t_recv.at[p]).wait()
 
         def widen(s, carry, p=p):
@@ -446,24 +452,6 @@
         for k in range(4):
             swap(p, k).start()
 
-    for kind in range(2):
-        for p in range(3):
-            pltpu.make_async_copy(
-                sbuf.at[kind, p, pl.ds(0, 7)], rbuf.at[kind, p, pl.ds(0, 7)], x_send.at[kind, p]
-            ).wait()
-    for way in range(2):
-        raw_copy(way).wait_send()
-        pltpu.make_async_copy(
-            raw.at[way, pl.ds(0, 7)], raw_in.at[way, pl.ds(0, 7)], v_send.at[way]
-        ).wait()
-    for step in range(1, 5):
-        for p in range(3):
-            for way in range(2):
-                if step > 1 or p > 0:
-                    ring_copy(way, step, p).wait_send()
-    for rel in range(2):
-        units = tsend.at[pl.ds(0, 45 if rel == 0 else 48)]
-        pltpu.make_async_copy(units, units, t_send.at[rel]).wait()
     for p in range(3):
         for k in range(4):
             swap(p, k).wait()

time: 73.2 us -> 71.4 us (0.975); the launches traced: 73.1 us -> 70.3 us
  Pallas kernels: 71.7 us -> 68.9 us
    pallas_call x1, Pallas kernels: 71.7 us -> 68.9 us  [per_device(): pl.pallas_call(kernel, out_shape=jax.ShapeDtypeStruct(pair.shape, BF16),...]
where the time goes in v5:
time: 71.4 us; the launch traced here: 70.3 us
  Pallas kernels  68.9 us (96%)
  local copies, waits for them, and re-layouts  1.41 us (2%)
    pallas_call x1, Pallas kernels, per_device(): pl.pallas_call(kernel, out_shape=jax.ShapeDtypeStruct(pair.shape, BF16),...  68.9 us

profile of v5, /device:TPU:5, one launch (start us, length us, event | category | flops | bytes accessed | tf_op | source)
XLA Modules:
  0.0 70.3 jit_solution(1776179366121425000)
XLA Ops:
  0.0 68.9 %shard_map.109 = bf16[48,192,128]{2,1,0:T(8,128)(2,1)S(1)} custom-call(bf16[48,192,128]{2,1,0:T(8,128)(2,1)} %refs_0_.1, f32[1,128]{1,0:T(1,128)} %bitcast.8, f32[1,128]{1,0:T(1,128)} %bitcast.9, bf16[128,512]{1,0:T(8,128)(2,1)} %refs_3_.1, f32[1,512]{1,0:T(1,128)} %bitcast.7, bf16[128,128]{1,0:T(8,128)(2,1)} %refs_5_.1, f32[1,128]{1,0:T(1,128)} %bitcast.10, ...), custom_call_target="tpu_custom_call" | custom-call | tf_op jit(solution)/shard_map/pallas_call | solution.py:489
  68.9 1.4 %copy.13 = bf16[48,192,128]{2,1,0:T(8,128)(2,1)} copy(bf16[48,192,128]{2,1,0:T(8,128)(2,1)S(1)} %shard_map.109) | data formatting | bytes 4718592

commit v6 on v5

--- a/solution.py
+++ b/solution.py
@@ -311,17 +311,19 @@
     project(2)
     pack(0, 2)
     exchange(0, 2)
-    for p in range(3):
-        pack(1, p)
+    pack(1, 0)
+    exchange(1, 0)
+    pack(1, 1)
+    exchange(1, 1)
+    pack(1, 2)
     unpack_right(1)
     start_ring(1)
     raw_spread(0)
     raw_spread(1)
     unpack_right(2)
     start_ring(2)
+    exchange(1, 2)
     exchange(0, 0)
-    for p in range(3):
-        exchange(1, p)
 
     mine = pl.ds(pl.multiple_of(core * 96, 96), 96)
 
@@ -343,29 +345,42 @@
     table[1] = jnp.broadcast_to(out_shift[...], (128, 128)).T
     table[2] = out_weight[...].astype(F32)
 
-    for step in range(1, 5):
-        plus = (z + 8 - step) % 8
-        minus = (z + step) % 8
-        for p in ORDER:
-            for way in range(2):
-                if step == 1 and p == 0:
-                    unpack_raw(way)
-                else:
-                    ring_copy(way, step, p).wait_recv()
-                if step < 4:
-                    ring_copy(way, step + 1, p).start()
-            if step > 1:
-                multiply(plus, p)
-                if step < 4:
-                    multiply(minus, p)
-        if step == 1:
-            unpack_right(0)
-            for p in range(3):
-                unpack_left(p)
-            for p in range(3):
-                multiply(z, p)
-                multiply(plus, p)
-                multiply(minus, p)
+    def forward(step, p):
+        for way in range(2):
+            if step == 1 and p == 0:
+                unpack_raw(way)
+            else:
+                ring_copy(way, step, p).wait_recv()
+            if step < 4:
+                ring_copy(way, step + 1, p).start()
+
+    def multiply_both(step, p):
+        multiply((z + 8 - step) % 8, p)
+        multiply((z + step) % 8, p)
+
+    for p in ORDER:
+        forward(1, p)
+    forward(2, 1)
+    forward(2, 2)
+    for p in range(3):
+        unpack_left(p)
+    unpack_right(0)
+    forward(2, 0)
+    for p in range(3):
+        multiply(z, p)
+        multiply_both(1, p)
+    forward(3, 1)
+    multiply_both(2, 1)
+    multiply_both(2, 2)
+    forward(3, 2)
+    multiply_both(2, 0)
+    multiply_both(3, 1)
+    forward(3, 0)
+    multiply_both(3, 2)
+    multiply_both(3, 0)
+    for p in ORDER:
+        forward(4, p)
+        multiply((z + 4) % 8, p)
 
     def regroup(n):
         return jnp.concatenate(

time: 71.4 us -> 73.6 us (1.031); the launches traced: 70.3 us -> 73.5 us
  Pallas kernels: 68.9 us -> 72.1 us
    pallas_call x1, Pallas kernels: 68.9 us -> 72.1 us  [per_device(): pl.pallas_call(kernel, out_shape=jax.ShapeDtypeStruct(pair.shape, BF16),...]
where the time goes in v6:
time: 73.6 us; the launch traced here: 73.5 us
  Pallas kernels  72.1 us (98%)
  local copies, waits for them, and re-layouts  1.41 us (2%)
    pallas_call x1, Pallas kernels, per_device(): pl.pallas_call(kernel, out_shape=jax.ShapeDtypeStruct(pair.shape, BF16),...  72.1 us

profile of v6, /device:TPU:5, one launch (start us, length us, event | category | flops | bytes accessed | tf_op | source)
XLA Modules:
  0.0 73.5 jit_solution(17026297709831272365)
XLA Ops:
  0.0 72.1 %shard_map.109 = bf16[48,192,128]{2,1,0:T(8,128)(2,1)S(1)} custom-call(bf16[48,192,128]{2,1,0:T(8,128)(2,1)} %refs_0_.1, f32[1,128]{1,0:T(1,128)} %bitcast.8, f32[1,128]{1,0:T(1,128)} %bitcast.9, bf16[128,512]{1,0:T(8,128)(2,1)} %refs_3_.1, f32[1,512]{1,0:T(1,128)} %bitcast.7, bf16[128,128]{1,0:T(8,128)(2,1)} %refs_5_.1, f32[1,128]{1,0:T(1,128)} %bitcast.10, ...), custom_call_target="tpu_custom_call" | custom-call | tf_op jit(solution)/shard_map/pallas_call | solution.py:504
  72.1 1.4 %copy.13 = bf16[48,192,128]{2,1,0:T(8,128)(2,1)} copy(bf16[48,192,128]{2,1,0:T(8,128)(2,1)S(1)} %shard_map.109) | data formatting | bytes 4718592

commit v7 on v5

--- a/solution.py
+++ b/solution.py
@@ -377,10 +377,17 @@
     weight = regroup(2).astype(BF16)
     group = lax.broadcasted_iota(jnp.int32, (32, 128), 1) // 32
 
-    def swap(p, k):
-        part = out.at[:, pl.ds(pl.multiple_of(core * 96 + k * 24 + p * 8, 8), 8), :]
+    def swap(p, half, k):
+        columns = pl.ds(pl.multiple_of(core * 96 + k * 24 + p * 8, 8), 8)
+        piece = out.at[pl.ds(half * 24, 24), columns, :]
         return remote(
-            part, part, o_send.at[p, k], o_recv.at[p, k], row, x, yl * 2 + 1 - core
+            piece,
+            piece,
+            o_send.at[p, half, k],
+            o_recv.at[p, half, k],
+            row,
+            x,
+            yl * 2 + 1 - core,
         )
 
     def drain():
@@ -415,7 +422,8 @@
 
         lax.fori_loop(0, 8, widen, 0, unroll=2)
 
-        def finish(g, carry, p=p):
+        def finish(n, carry, half):
+            g = (n // 2) * 4 + half * 2 + n % 2
             from_row = [wide[pl.ds(g * 4 + i, 32, stride=48), :] for i in range(4)]
             blocks = []
             for c in range(4):
@@ -429,16 +437,15 @@
             centred = vals - jnp.mean(vals, axis=0, keepdims=True)
             spread = jnp.mean(centred * centred, axis=0, keepdims=True)
             rows = (centred * lax.rsqrt(spread + EPS) * gains + shifts).astype(BF16)
-            normal[pl.ds(pl.multiple_of(g * 128, 128), 128), :] = rows.T
+            at = pl.ds(pl.multiple_of(half * 768 + n * 128, 128), 128)
+            normal[at, :] = rows.T
             return carry
 
-        lax.fori_loop(0, 12, finish, 0, unroll=UNROLL)
-
-        def apply(g, carry, p=p):
-            rows = normal[pl.ds(pl.multiple_of(g * 256, 256), 256), :]
+        def apply(n, carry, half, p=p):
+            rows = normal[pl.ds(pl.multiple_of(half * 768 + n * 256, 256), 256), :]
             projected = jnp.dot(rows, weight, preferred_element_type=F32) + out_bias[...]
             for i in range(8):
-                line = (g % 2) * 24 + (g // 2) * 8 + i
+                line = half * 24 + n * 8 + i
                 for k in range(4):
                     j = k * 24 + p * 8
                     value = (
@@ -448,13 +455,16 @@
                     out[line, pl.ds(pl.multiple_of(core * 96 + j, 8), 8), :] = value.astype(BF16)
             return carry
 
-        lax.fori_loop(0, 6, apply, 0, unroll=2)
-        for k in range(4):
-            swap(p, k).start()
+        for half in range(2):
+            lax.fori_loop(0, 6, functools.partial(finish, half=half), 0, unroll=UNROLL)
+            lax.fori_loop(0, 3, functools.partial(apply, half=half), 0, unroll=3)
+            for k in range(4):
+                swap(p, half, k).start()
 
     for p in range(3):
-        for k in range(4):
-            swap(p, k).wait()
+        for half in range(2):
+            for k in range(4):
+                swap(p, half, k).wait()
 
 
 def per_device(
@@ -524,8 +534,8 @@
             dma((2, 3)),
             dma((2,)),
             dma((3,)),
-            dma((3, 4)),
-            dma((3, 4)),
+            dma((3, 2, 4)),
+            dma((3, 2, 4)),
         ],
         compiler_params=pltpu.CompilerParams(
             collective_id=0, has_side_effects=True, vmem_limit_bytes=VMEM_MIB * 1024 * 1024

time: 71.4 us -> 70.3 us (0.985)
  Pallas kernels: 68.9 us -> 68.1 us
    pallas_call x1, Pallas kernels: 68.9 us -> 68.1 us  [per_device(): pl.pallas_call(kernel, out_shape=jax.ShapeDtypeStruct(pair.shape, BF16),...]
where the time goes in v7:
time: 70.3 us; the launch traced here: 69.6 us
  Pallas kernels  68.1 us (97%)
  local copies, waits for them, and re-layouts  1.41 us (2%)
    pallas_call x1, Pallas kernels, per_device(): pl.pallas_call(kernel, out_shape=jax.ShapeDtypeStruct(pair.shape, BF16),...  68.1 us
    unnamed x1, local copies, waits for them, and re-layouts  1.41 us

profile of v7, /device:TPU:5, one launch (start us, length us, event | category | flops | bytes accessed | tf_op | source)
XLA Modules:
  0.0 69.6 jit_solution(16643217717274678033)
XLA Ops:
  0.0 68.1 %shard_map.109 = bf16[48,192,128]{2,1,0:T(8,128)(2,1)S(1)} custom-call(bf16[48,192,128]{2,1,0:T(8,128)(2,1)} %refs_0_.1, f32[1,128]{1,0:T(1,128)} %bitcast.8, f32[1,128]{1,0:T(1,128)} %bitcast.9, bf16[128,512]{1,0:T(8,128)(2,1)} %refs_3_.1, f32[1,512]{1,0:T(1,128)} %bitcast.7, bf16[128,128]{1,0:T(8,128)(2,1)} %refs_5_.1, f32[1,128]{1,0:T(1,128)} %bitcast.10, ...), custom_call_target="tpu_custom_call" | custom-call | tf_op jit(solution)/shard_map/pallas_call | solution.py:499
  68.1 1.4 %copy.13 = bf16[48,192,128]{2,1,0:T(8,128)(2,1)} copy(bf16[48,192,128]{2,1,0:T(8,128)(2,1)S(1)} %shard_map.109) | data formatting | bytes 4718592

commit v8 on v7

--- a/solution.py
+++ b/solution.py
@@ -305,23 +305,25 @@
     project(1)
     pack(0, 1)
     pl.semaphore_wait(barrier, 33)
+    exchange(0, 1)
     raw_copy(0).start()
     raw_copy(1).start()
-    exchange(0, 1)
     project(2)
     pack(0, 2)
     exchange(0, 2)
-    for p in range(3):
-        pack(1, p)
+    pack(1, 0)
+    exchange(1, 0)
+    pack(1, 1)
+    exchange(1, 1)
+    pack(1, 2)
     unpack_right(1)
     start_ring(1)
     raw_spread(0)
     raw_spread(1)
     unpack_right(2)
     start_ring(2)
+    exchange(1, 2)
     exchange(0, 0)
-    for p in range(3):
-        exchange(1, p)
 
     mine = pl.ds(pl.multiple_of(core * 96, 96), 96)
 
@@ -354,6 +356,9 @@
                     ring_copy(way, step, p).wait_recv()
                 if step < 4:
                     ring_copy(way, step + 1, p).start()
+            if step == 2:
+                multiply((z + 7) % 8, p)
+                multiply((z + 1) % 8, p)
             if step > 1:
                 multiply(plus, p)
                 if step < 4:
@@ -364,8 +369,6 @@
                 unpack_left(p)
             for p in range(3):
                 multiply(z, p)
-                multiply(plus, p)
-                multiply(minus, p)
 
     def regroup(n):
         return jnp.concatenate(

time: 70.3 us -> 70.2 us (level)
  no operation moved by 1% of the time
where the time goes in v8:
time: 70.2 us; the launch traced here: 69.6 us
  Pallas kernels  68.2 us (97%)
  local copies, waits for them, and re-layouts  1.41 us (2%)
    pallas_call x1, Pallas kernels, per_device(): pl.pallas_call(kernel, out_shape=jax.ShapeDtypeStruct(pair.shape, BF16),...  68.2 us
    unnamed x1, local copies, waits for them, and re-layouts  1.41 us

profile of v8, /device:TPU:5, one launch (start us, length us, event | category | flops | bytes accessed | tf_op | source)
XLA Modules:
  0.0 69.6 jit_solution(16385946115559176458)
XLA Ops:
  0.0 68.2 %shard_map.109 = bf16[48,192,128]{2,1,0:T(8,128)(2,1)S(1)} custom-call(bf16[48,192,128]{2,1,0:T(8,128)(2,1)} %refs_0_.1, f32[1,128]{1,0:T(1,128)} %bitcast.8, f32[1,128]{1,0:T(1,128)} %bitcast.9, bf16[128,512]{1,0:T(8,128)(2,1)} %refs_3_.1, f32[1,512]{1,0:T(1,128)} %bitcast.7, bf16[128,128]{1,0:T(8,128)(2,1)} %refs_5_.1, f32[1,128]{1,0:T(1,128)} %bitcast.10, ...), custom_call_target="tpu_custom_call" | custom-call | tf_op jit(solution)/shard_map/pallas_call | solution.py:502
  68.2 1.4 %copy.13 = bf16[48,192,128]{2,1,0:T(8,128)(2,1)} copy(bf16[48,192,128]{2,1,0:T(8,128)(2,1)S(1)} %shard_map.109) | data formatting | bytes 4718592
